TPU v7x, 32 devices: a whole 2x2x4 slice. The times are simulated.
32 devices in a mesh: row: 16 (over z, x, core), blk: 2 (over y).
Axes of the slice: x: 2, y: 2, z: 4, core: 2. Of those that a mesh axis runs over, the one named last changes fastest.
Arguments:
- embeddings: bfloat16 [8192, 192], P(('row', 'blk')), may hold values from -30 to 30
- vectors: float32 [8192, 16], P(('row', 'blk')), may hold values from -6 to 6
Outputs:
- basis: float32 [8192, 16], P(('row', 'blk'))
- triangle: float32 [16, 16], replicated
All inputs are finite; a program needn't handle non-finite values.
Results may differ from a plain program's by a relative error of at most 0.0088.
Values may be sent and summed in bfloat16 or wider, within the bound.
A program may use at most 64 MiB of HBM per device.

v0:
```python
import jax
import jax.numpy as jnp
from jax import lax
from jax.sharding import PartitionSpec as P

sharpness = 10.0
epsilon = 1e-06


def normalize(embeddings):
    values = embeddings.astype(jnp.float32)
    return (values * lax.rsqrt(jnp.sum(values * values, axis=1, keepdims=True) + epsilon)).astype(
        jnp.bfloat16
    )


def affinity(block_rows, columns):
    scores = lax.dot_general(
        block_rows, columns, (((1,), (1,)), ((), ())), preferred_element_type=jnp.float32
    )
    return jnp.exp(sharpness * (scores - 1.0))


def gram_total(projected):
    local_gram = jnp.dot(projected.T, projected, precision=lax.Precision.HIGHEST)
    return lax.psum(local_gram, ("row", "blk"))


def finish(projected, gram_matrix):
    factor = jnp.linalg.cholesky(gram_matrix)
    basis = jax.scipy.linalg.solve_triangular(factor, projected.T, lower=True).T
    return (basis, factor.T)


def per_device(embeddings, vectors):
    unit_rows = normalize(embeddings)
    local_rows = unit_rows.shape[0]
    columns_out = vectors.shape[1]
    everything = lax.all_gather(unit_rows, ("row", "blk"), axis=0, tiled=True)
    column_blocks = everything.reshape(16, -1, everything.shape[1])

    def add_degree(running, columns):
        return (running + jnp.sum(affinity(unit_rows, columns), axis=1), None)

    degree, unused = lax.scan(add_degree, jnp.zeros((local_rows,), jnp.float32), column_blocks)
    inverse_root = lax.rsqrt(degree)
    weighted = (vectors * inverse_root[:, None]).astype(jnp.bfloat16)
    all_weighted = lax.all_gather(weighted, ("row", "blk"), axis=0, tiled=True)
    weight_blocks = all_weighted.reshape(16, -1, columns_out)

    def add_image(running, column_pair):
        tile = affinity(unit_rows, column_pair[0]).astype(jnp.bfloat16)
        return (running + jnp.dot(tile, column_pair[1], preferred_element_type=jnp.float32), None)

    summed, unused = lax.scan(
        add_image, jnp.zeros((local_rows, columns_out), jnp.float32), (column_blocks, weight_blocks)
    )
    projected = summed * inverse_root[:, None]
    gram_matrix = gram_total(projected)
    return finish(projected, gram_matrix)


def solution(mesh):
    placed = (P(("row", "blk"), None), P(("row", "blk"), None))
    return jax.shard_map(
        per_device,
        mesh=mesh,
        in_specs=placed,
        out_specs=(P(("row", "blk"), None), P()),
        check_vma=False,
    )
```

profile of v0, /device:TPU:10, one launch (start us, length us, event | category | flops | bytes accessed | tf_op | source)
XLA Modules:
  0.0 237.3 jit_solution(9475091258592382301)
XLA Ops:
  7.2 0.0 copy-start
  7.2 0.0 all-gather.2.cloned.1.call-start
  7.2 1.0 copy.4
  8.2 0.1 fusion.23
  8.3 0.8 fusion.24
  9.1 0.0 all-gather.2.cloned.1.call-update
  9.1 64.3 %all-gather.2.cloned.1.call-done = bf16[8192,192]{1,0:T(8,128)(2,1)} async-done(((bf16[256,192]{1,0:T(8,128)(2,1)}), bf16[8192,192]{1,0:T(8,128)(2,1)}) %all-gather.2.cloned.1.call-update) | async-done | bytes 3145744 | tf_op jit(solution)/shard_map/all_gather | solution.py:39
  73.5 21.6 %while.26 = (s32[]{:T(128)}, f32[256]{0:T(256)S(1)}, bf16[16,512,192]{2,1,0:T(8,128)(2,1)}, bf16[256,192]{1,0:T(8,128)(2,1)}, s32[]{:T(128)}, /*index=5*/s32[]{:T(128)}) while((s32[]{:T(128)}, f32[256]{0:T(256)S(1)}, bf16[16,512,192]{2,1,0:T(8,128)(2,1)}, bf16[256,192]{1,0:T(8,128)(2,1)}, s32[]{:T(128)}, /*index=5*/s32[]{:T(128)}) %tuple.72), condition=%wide.region_3.4_spmd.clone, body=%wide.region_1.3_spmd.clone.sunk | while | flops 50725120 | bytes 397903 | solution.py:45
  73.5 1.3 fusion.45
  74.8 1.3 fusion.45
  76.2 1.3 fusion.45
  77.5 1.3 fusion.45
  78.9 1.3 fusion.45
  80.2 1.3 fusion.45
  81.6 1.3 fusion.45
  82.9 1.3 fusion.45
  84.3 1.3 fusion.45
  85.6 1.3 fusion.45
  87.0 1.3 fusion.45
  88.3 1.3 fusion.45
  89.7 1.3 fusion.45
  91.0 1.3 fusion.45
  92.4 1.3 fusion.45
  93.7 1.3 fusion.45
  95.1 0.0 copy-done
  95.1 48.5 %all_gather.7 = bf16[8192,16]{0,1:T(8,128)(2,1)S(1)} all-gather(bf16[256,16]{0,1:T(8,128)(2,1)S(1)} %multiply_convert_fusion), channel_id=1, replica_groups=mesh['row'=16,'blk'=2] {'row','blk'}, dimensions={0}, use_global_device_ids=true | all-gather | bytes 270336 | tf_op jit(solution)/shard_map/all_gather | solution.py:48
  143.6 22.8 %while.27 = (s32[]{:T(128)}, f32[256,16]{0,1:T(8,128)S(1)}, bf16[16,512,192]{2,1,0:T(8,128)(2,1)}, bf16[256,192]{1,0:T(8,128)(2,1)}, bf16[16,512,16]{1,2,0:T(8,128)(2,1)S(1)}, /*index=5*/s32[]{:T(128)}, s32[]{:T(128)}) while((s32[]{:T(128)}, f32[256,16]{0,1:T(8,128)S(1)}, bf16[16,512,192]{2,1,0:T(8,128)(2,1)}, ...), condition=%wide.region_5.6_spmd.clone, body=%wide.region_4.5_spmd.clone.sunk | while | flops 54927360 | bytes 443479 | solution.py:55
  143.6 1.4 fusion.49
  145.0 1.4 fusion.49
  146.4 1.4 fusion.49
  147.9 1.4 fusion.49
  149.3 1.4 fusion.49
  150.7 1.4 fusion.49
  152.1 1.4 fusion.49
  153.6 1.4 fusion.49
  155.0 1.4 fusion.49
  156.4 1.4 fusion.49
  157.8 1.4 fusion.49
  159.3 1.4 fusion.49
  160.7 1.4 fusion.49
  162.1 1.4 fusion.49
  163.5 1.4 fusion.49
  165.0 1.4 fusion.49
  166.4 0.1 fusion.27
  166.5 58.4 %psum.7 = f32[16,16]{0,1:T(8,128)S(1)} all-reduce(f32[16,16]{0,1:T(8,128)S(1)} %fusion.27), channel_id=1, replica_groups=mesh['row'=16,'blk'=2] {'row','blk'}, use_global_device_ids=true, to_apply=%region_6.7 | all-reduce | flops 256 | bytes 2048 | tf_op jit(solution)/shard_map/psum | solution.py:26
  224.9 0.1 copy.7
  225.0 1.5 cholesky.16
  226.4 0.6 compare_reduce_fusion
  227.1 0.6 fusion.33
  227.7 1.2 custom-call.7
  229.0 0.8 fusion.25
  229.8 0.7 copy.8
  (24 shorter events, 0.3 us)
Async XLA Ops:
  7.2 87.9 %copy-start = (f32[256,16]{0,1:T(8,128)S(1)}, f32[256,16]{0,1:T(8,128)}, u32[]{:S(2)}) copy-start(f32[256,16]{0,1:T(8,128)} %param.7) | copy-start | bytes 49156
  7.2 66.3 %all-gather.2.cloned.1.call-start = ((), (), s32[]{:S(2)}) async-start(), calls=%async_computation | async-start | bytes 4325376 | tf_op jit(solution)/shard_map/all_gather | solution.py:39
Sparse Core Ops, SparseCore 0:
  10.9 62.5 all-gather.1
where the time goes:
time: 238 us; the launch traced here: 237 us
  blocking collectives  107 us (45%)
  waiting for transfers between devices  64.4 us (27%)
  matrix products  44.8 us (19%)
  between operations  14.1 us (6%)
  other arithmetic  5.09 us (2%)
    all_gather x1, waiting for transfers between devices, per_device(): everything = lax.all_gather(unit_rows, ('row', 'blk'), axis=0, tiled=True)  64.3 us
    psum x1, blocking collectives, gram_total(): return lax.psum(local_gram, ('row', 'blk'))  58.4 us
    all_gather x1, blocking collectives, per_device(): all_weighted = lax.all_gather(weighted, ('row', 'blk'), axis=0, tiled=True)  48.5 us
    dot_general x16, matrix products, add_image(): jnp.dot(tile, column_pair[1], preferred_element_type=jnp.float32)  22.8 us
    dot_general x16, matrix products, affinity(): lax.dot_general(block_rows, columns, (((1,), (1,)), ((), ())), preferred_...  21.1 us
  transfers between devices with their start and end apart: 1, of which 1 were waited for; matrix products, arithmetic and copies ran while one was open for 0% of the time, Pallas kernels for 0%

commit v1 on v0

--- a/solution.py
+++ b/solution.py
@@ -23,7 +23,7 @@
 
 def gram_total(projected):
     local_gram = jnp.dot(projected.T, projected, precision=lax.Precision.HIGHEST)
-    return lax.psum(local_gram, ("row", "blk"))
+    return jnp.sum(lax.all_gather(local_gram, ("row", "blk")), axis=0)
 
 
 def finish(projected, gram_matrix):

time: 238 us -> 265 us (1.11)
  the two profiles are of different devices: /device:TPU:10 before, /device:TPU:0 now
where the time goes in v1:
time: 265 us
  blocking collectives  132 us (50%)
  waiting for transfers between devices  66.2 us (25%)
  matrix products  44.8 us (17%)
  between operations  14.1 us (5%)
  other arithmetic  5.12 us (2%)
    all_gather x1, blocking collectives, per_device(): all_weighted = lax.all_gather(weighted, ('row', 'blk'), axis=0, tiled=True)  67.5 us
    all_gather x1, waiting for transfers between devices, per_device(): everything = lax.all_gather(unit_rows, ('row', 'blk'), axis=0, tiled=True)  66.2 us
    all_gather x1, blocking collectives, gram_total(): return jnp.sum(lax.all_gather(local_gram, ('row', 'blk')), axis=0)  64.7 us
    dot_general x16, matrix products, add_image(): jnp.dot(tile, column_pair[1], preferred_element_type=jnp.float32)  22.8 us
    dot_general x16, matrix products, affinity(): lax.dot_general(block_rows, columns, (((1,), (1,)), ((), ())), preferred_...  21.1 us
  transfers between devices with their start and end apart: 1, of which 1 were waited for; matrix products, arithmetic and copies ran while one was open for 0% of the time, Pallas kernels for 0%

profile of v1, /device:TPU:0, one launch (start us, length us, event | category | flops | bytes accessed | tf_op | source)
XLA Modules:
  0.0 264.6 jit_solution(17470006386670815679)
XLA Ops:
  7.2 0.0 copy-start
  7.2 0.0 all-gather.3.cloned.1.call-start
  7.2 1.0 copy.8
  8.2 0.1 fusion.23
  8.3 0.8 fusion.24
  9.1 0.0 all-gather.3.cloned.1.call-update
  9.1 66.2 %all-gather.3.cloned.1.call-done = bf16[8192,192]{1,0:T(8,128)(2,1)} async-done(((bf16[256,192]{1,0:T(8,128)(2,1)}), bf16[8192,192]{1,0:T(8,128)(2,1)}) %all-gather.3.cloned.1.call-update) | async-done | bytes 3145744 | tf_op jit(solution)/shard_map/all_gather | solution.py:39
  75.3 21.6 %while.26 = (s32[]{:T(128)}, f32[256]{0:T(256)S(1)}, bf16[16,512,192]{2,1,0:T(8,128)(2,1)}, bf16[256,192]{1,0:T(8,128)(2,1)}, s32[]{:T(128)}, /*index=5*/s32[]{:T(128)}) while((s32[]{:T(128)}, f32[256]{0:T(256)S(1)}, bf16[16,512,192]{2,1,0:T(8,128)(2,1)}, bf16[256,192]{1,0:T(8,128)(2,1)}, s32[]{:T(128)}, /*index=5*/s32[]{:T(128)}) %tuple.74), condition=%wide.region_3.4_spmd.clone, body=%wide.region_1.3_spmd.clone.sunk | while | flops 50725120 | bytes 397903 | solution.py:45
  75.3 1.3 fusion.45
  76.7 1.3 fusion.45
  78.0 1.3 fusion.45
  79.4 1.3 fusion.45
  80.7 1.3 fusion.45
  82.1 1.3 fusion.45
  83.4 1.3 fusion.45
  84.8 1.3 fusion.45
  86.1 1.3 fusion.45
  87.5 1.3 fusion.45
  88.8 1.3 fusion.45
  90.2 1.3 fusion.45
  91.5 1.3 fusion.45
  92.9 1.3 fusion.45
  94.2 1.3 fusion.45
  95.6 1.3 fusion.45
  96.9 0.0 copy-done
  96.9 67.5 %all_gather.13 = bf16[8192,16]{0,1:T(8,128)(2,1)S(1)} all-gather(bf16[256,16]{0,1:T(8,128)(2,1)S(1)} %multiply_convert_fusion), channel_id=1, replica_groups=mesh['row'=16,'blk'=2] {'row','blk'}, dimensions={0}, use_global_device_ids=true | all-gather | bytes 270336 | tf_op jit(solution)/shard_map/all_gather | solution.py:48
  164.5 22.8 %while.27 = (s32[]{:T(128)}, f32[256,16]{0,1:T(8,128)S(1)}, bf16[16,512,192]{2,1,0:T(8,128)(2,1)}, bf16[256,192]{1,0:T(8,128)(2,1)}, bf16[16,512,16]{1,2,0:T(8,128)(2,1)S(1)}, /*index=5*/s32[]{:T(128)}, s32[]{:T(128)}) while((s32[]{:T(128)}, f32[256,16]{0,1:T(8,128)S(1)}, bf16[16,512,192]{2,1,0:T(8,128)(2,1)}, ...), condition=%wide.region_5.6_spmd.clone, body=%wide.region_4.5_spmd.clone.sunk | while | flops 54927360 | bytes 443479 | solution.py:55
  164.5 1.4 fusion.49
  165.9 1.4 fusion.49
  167.4 1.4 fusion.49
  168.8 1.4 fusion.49
  170.2 1.4 fusion.49
  171.6 1.4 fusion.49
  173.1 1.4 fusion.49
  174.5 1.4 fusion.49
  175.9 1.4 fusion.49
  177.3 1.4 fusion.49
  178.7 1.4 fusion.49
  180.2 1.4 fusion.49
  181.6 1.4 fusion.49
  183.0 1.4 fusion.49
  184.4 1.4 fusion.49
  185.9 1.4 fusion.49
  187.3 0.1 fusion.27
  187.4 64.7 %all-gather = f32[512,16]{1,0:T(8,128)S(1)} all-gather(f32[16,16]{1,0:T(8,128)S(1)} %fusion.27), channel_id=2, replica_groups=mesh['row'=16,'blk'=2] {'row','blk'}, dimensions={0}, use_global_device_ids=true | all-gather | bytes 33792 | tf_op jit(solution)/shard_map/all_gather | solution.py:26
  252.2 0.1 copy.10
  252.3 1.5 cholesky.16
  253.7 0.6 compare_reduce_fusion
  254.4 0.6 fusion.33
  255.1 1.2 custom-call.7
  256.3 0.8 fusion.25
  257.1 0.7 copy.11
  (25 shorter events, 0.3 us)
Async XLA Ops:
  7.2 89.8 %copy-start = (f32[256,16]{0,1:T(8,128)S(1)}, f32[256,16]{0,1:T(8,128)}, u32[]{:S(2)}) copy-start(f32[256,16]{0,1:T(8,128)} %param.7) | copy-start | bytes 49156
  7.2 68.2 %all-gather.3.cloned.1.call-start = ((), (), s32[]{:S(2)}) async-start(), calls=%async_computation | async-start | bytes 4325376 | tf_op jit(solution)/shard_map/all_gather | solution.py:39
Sparse Core Ops, SparseCore 0:
  10.9 64.4 all-gather.2

commit v2 on v0

--- a/solution.py
+++ b/solution.py
@@ -36,7 +36,15 @@
     unit_rows = normalize(embeddings)
     local_rows = unit_rows.shape[0]
     columns_out = vectors.shape[1]
-    everything = lax.all_gather(unit_rows, ("row", "blk"), axis=0, tiled=True)
+    ways, here = (lax.axis_size(("row", "blk")), lax.axis_index(("row", "blk")))
+    grown, reach = (unit_rows, 1)
+    while reach < ways:
+        theirs = lax.ppermute(grown, ("row", "blk"), [(d, d ^ reach) for d in range(ways)])
+        mine_first = jnp.concatenate([grown, theirs], axis=0)
+        theirs_first = jnp.concatenate([theirs, grown], axis=0)
+        grown = jnp.where(here & reach == 0, mine_first, theirs_first)
+        reach = 2 * reach
+    everything = grown
     column_blocks = everything.reshape(16, -1, everything.shape[1])
 
     def add_degree(running, columns):

time: 238 us -> 276 us (1.16)
  waiting for transfers between devices: 64.4 us -> 99.1 us
  between operations: 14.1 us -> 0.78 us
  other arithmetic: 5.09 us -> 10.7 us
  starting transfers between devices: 0.04 us -> 5.42 us
  local copies, waits for them, and re-layouts: 1.75 us -> 4.75 us
  blocking collectives: 107 us -> 110 us
    ppermute x0 -> x5, waiting for transfers between devices: none -> 99.1 us  [per_device(): lax.ppermute(grown, ('row', 'blk'), [(d, d ^ reach) for d in range(ways)])]
    all_gather x1 -> x0, waiting for transfers between devices: 64.3 us -> none  [per_device(): everything = lax.all_gather(unit_rows, ('row', 'blk'), axis=0, tiled=True)]
    ppermute x0 -> x5, starting transfers between devices: none -> 5.42 us  [per_device(): lax.ppermute(grown, ('row', 'blk'), [(d, d ^ reach) for d in range(ways)])]
    select_n x0 -> x5, other arithmetic: none -> 4.66 us  [per_device(): grown = jnp.where(here & reach == 0, mine_first, theirs_first)]
    unnamed x4 -> x7, local copies, waits for them, and re-layouts: 1.66 us -> 4.66 us
  transfers between devices with their start and end apart: 1 -> 5, of which waited for: 1 -> 5; matrix products, arithmetic and copies ran while one was open for 0% -> 0% of each run, Pallas kernels for 0% -> 0%
where the time goes in v2:
time: 276 us; the launch traced here: 274 us
  blocking collectives  110 us (40%)
  waiting for transfers between devices  99.1 us (36%)
  matrix products  43.7 us (16%)
  other arithmetic  10.7 us (4%)
  starting transfers between devices  5.42 us (2%)
  local copies, waits for them, and re-layouts  4.75 us (2%)
    ppermute x5, waiting for transfers between devices, per_device(): lax.ppermute(grown, ('row', 'blk'), [(d, d ^ reach) for d in range(ways)])  99.1 us
    psum x1, blocking collectives, gram_total(): return lax.psum(local_gram, ('row', 'blk'))  59.6 us
    all_gather x1, blocking collectives, per_device(): all_weighted = lax.all_gather(weighted, ('row', 'blk'), axis=0, tiled=True)  50 us
    dot_general x16, matrix products, add_image(): jnp.dot(tile, column_pair[1], preferred_element_type=jnp.float32)  22.2 us
    dot_general x16, matrix products, affinity(): lax.dot_general(block_rows, columns, (((1,), (1,)), ((), ())), preferred_...  20.5 us
  transfers between devices with their start and end apart: 5, of which 5 were waited for; matrix products, arithmetic and copies ran while one was open for 0% of the time, Pallas kernels for 0%

profile of v2, /device:TPU:10, one launch (start us, length us, event | category | flops | bytes accessed | tf_op | source)
XLA Modules:
  0.0 274.5 jit_solution(15880969397334541634)
XLA Ops:
  0.6 0.9 fusion.23
  1.6 0.9 fusion.24
  2.5 1.6 collective-permute-start
  4.1 3.1 %collective-permute-done = bf16[256,192]{0,1:T(8,128)(2,1)S(1)} collective-permute-done((bf16[256,192]{0,1:T(8,128)(2,1)S(1)}, bf16[256,192]{0,1:T(8,128)(2,1)S(1)}, u32[]{:S(2)}, u32[]{:S(2)}) %collective-permute-start) | collective-permute-done | bytes 98336 | tf_op jit(solution)/shard_map/ppermute | solution.py:42
  7.2 0.1 maximum_select_fusion.4
  7.3 0.1 collective-permute-start.1
  7.3 1.4 collective-permute-done.1
  8.8 0.1 maximum_select_fusion.3
  8.9 0.6 collective-permute-start.2
  9.5 10.6 %collective-permute-done.2 = bf16[1024,192]{0,1:T(8,128)(2,1)S(1)} collective-permute-done((bf16[1024,192]{0,1:T(8,128)(2,1)S(1)}, bf16[1024,192]{0,1:T(8,128)(2,1)S(1)}, u32[]{:S(2)}, u32[]{:S(2)}) %collective-permute-start.2) | collective-permute-done | bytes 393248 | tf_op jit(solution)/shard_map/ppermute | solution.py:42
  20.1 0.3 maximum_select_fusion.2
  20.4 0.5 collective-permute-start.3
  20.9 18.3 %collective-permute-done.3 = bf16[2048,192]{0,1:T(8,128)(2,1)S(1)} collective-permute-done((bf16[2048,192]{0,1:T(8,128)(2,1)S(1)}, bf16[2048,192]{0,1:T(8,128)(2,1)S(1)}, u32[]{:S(2)}, u32[]{:S(2)}) %collective-permute-start.3) | collective-permute-done | bytes 786464 | tf_op jit(solution)/shard_map/ppermute | solution.py:42
  39.2 0.5 maximum_select_fusion.1
  39.7 2.7 collective-permute-start.4
  42.4 0.1 copy.12
  42.5 65.7 %collective-permute-done.4 = bf16[4096,192]{0,1:T(8,128)(2,1)} collective-permute-done((bf16[4096,192]{0,1:T(8,128)(2,1)S(1)}, bf16[4096,192]{0,1:T(8,128)(2,1)}, u32[]{:S(2)}, u32[]{:S(2)}) %collective-permute-start.4) | collective-permute-done | bytes 1572896 | tf_op jit(solution)/shard_map/ppermute | solution.py:42
  108.2 3.7 %maximum_select_fusion = bf16[8192,192]{0,1:T(8,128)(2,1)S(1)} fusion(bf16[4096,192]{0,1:T(8,128)(2,1)} %collective-permute-done.4, bf16[4096,192]{0,1:T(8,128)(2,1)} %copy-done, pred[]{:T(512)S(6)} %eq.15), kind=kLoop, calls=%fused_computation.23 | loop fusion | flops 14155776 | bytes 6291457 | tf_op jit(solution)/shard_map/jit(_where)/select_n | solution.py:45
  111.9 3.9 %copy.18 = bf16[8192,192]{1,0:T(8,128)(2,1)} copy(bf16[8192,192]{0,1:T(8,128)(2,1)S(1)} %maximum_select_fusion) | data formatting | bytes 6291456
  115.8 21.0 %while.26 = (s32[]{:T(128)}, f32[256]{0:T(256)S(1)}, bf16[16,512,192]{2,1,0:T(8,128)(2,1)}, bf16[256,192]{1,0:T(8,128)(2,1)S(1)}, s32[]{:T(128)}, /*index=5*/s32[]{:T(128)}) while((s32[]{:T(128)}, f32[256]{0:T(256)S(1)}, bf16[16,512,192]{2,1,0:T(8,128)(2,1)}, bf16[256,192]{1,0:T(8,128)(2,1)S(1)}, s32[]{:T(128)}, ...), condition=%wide.region_3.4_spmd.clone, body=%wide.region_1.3_spmd.clone.sunk | while | flops 50725120 | bytes 365135 | solution.py:53
  115.8 1.3 fusion.45
  117.1 1.3 fusion.45
  118.4 1.3 fusion.45
  119.7 1.3 fusion.45
  121.1 1.3 fusion.45
  122.4 1.3 fusion.45
  123.7 1.3 fusion.45
  125.0 1.3 fusion.45
  126.3 1.3 fusion.45
  127.6 1.3 fusion.45
  129.0 1.3 fusion.45
  130.3 1.3 fusion.45
  131.6 1.3 fusion.45
  132.9 1.3 fusion.45
  134.2 1.3 fusion.45
  135.5 1.3 fusion.45
  136.9 0.0 copy-done.1
  136.9 50.0 %all_gather.3 = bf16[8192,16]{0,1:T(8,128)(2,1)S(1)} all-gather(bf16[256,16]{0,1:T(8,128)(2,1)S(1)} %multiply_convert_fusion), channel_id=1, replica_groups=mesh['row'=16,'blk'=2] {'row','blk'}, dimensions={0}, use_global_device_ids=true | all-gather | bytes 270336 | tf_op jit(solution)/shard_map/all_gather | solution.py:56
  186.9 22.2 %while.27 = (s32[]{:T(128)}, f32[256,16]{0,1:T(8,128)S(1)}, bf16[16,512,192]{2,1,0:T(8,128)(2,1)}, bf16[256,192]{1,0:T(8,128)(2,1)S(1)}, bf16[16,512,16]{1,2,0:T(8,128)(2,1)S(1)}, /*index=5*/s32[]{:T(128)}, s32[]{:T(128)}) while((s32[]{:T(128)}, f32[256,16]{0,1:T(8,128)S(1)}, bf16[16,512,192]{2,1,0:T(8,128)(2,1)}, ...), condition=%wide.region_5.6_spmd.clone, body=%wide.region_4.5_spmd.clone.sunk | while | flops 54927360 | bytes 443479 | solution.py:63
  186.9 1.4 fusion.49
  188.3 1.4 fusion.49
  189.7 1.4 fusion.49
  191.1 1.4 fusion.49
  192.4 1.4 fusion.49
  193.8 1.4 fusion.49
  195.2 1.4 fusion.49
  196.6 1.4 fusion.49
  198.0 1.4 fusion.49
  199.4 1.4 fusion.49
  200.8 1.4 fusion.49
  202.2 1.4 fusion.49
  203.6 1.4 fusion.49
  205.0 1.4 fusion.49
  206.3 1.4 fusion.49
  207.7 1.4 fusion.49
  209.1 0.1 fusion.27
  209.3 59.6 %psum.7 = f32[16,16]{0,1:T(8,128)S(1)} all-reduce(f32[16,16]{0,1:T(8,128)S(1)} %fusion.27), channel_id=1, replica_groups=mesh['row'=16,'blk'=2] {'row','blk'}, use_global_device_ids=true, to_apply=%region_6.7 | all-reduce | flops 256 | bytes 2048 | tf_op jit(solution)/shard_map/psum | solution.py:26
  268.9 0.1 copy.15
  269.0 1.5 cholesky.16
  270.5 0.6 compare_reduce_fusion
  271.1 0.6 fusion.33
  271.8 1.2 custom-call.7
  273.0 0.8 fusion.25
  273.8 0.7 copy.16
  (27 shorter events, 0.3 us)
Async XLA Ops:
  2.5 4.7 %collective-permute-start = (bf16[256,192]{0,1:T(8,128)(2,1)S(1)}, bf16[256,192]{0,1:T(8,128)(2,1)S(1)}, u32[]{:S(2)}, u32[]{:S(2)}) collective-permute-start(bf16[256,192]{0,1:T(8,128)(2,1)S(1)} %fusion.24), channel_id=1, source_target_pairs={{0,1},{1,0},{2,3},{3,2},{4,5},{5,4},{6,7},{7,6},{8,9},{9,8},{10,11... | collective-permute-start | bytes 294920 | tf_op jit(solution)/shard_map/ppermute | solution.py:42
  7.3 1.5 collective-permute-start.1
  8.9 11.2 %collective-permute-start.2 = (bf16[1024,192]{0,1:T(8,128)(2,1)S(1)}, bf16[1024,192]{0,1:T(8,128)(2,1)S(1)}, u32[]{:S(2)}, u32[]{:S(2)}) collective-permute-start(bf16[1024,192]{0,1:T(8,128)(2,1)S(1)} %maximum_select_fusion.3), channel_id=1, source_target_pairs={{0,4},{1,5},{2,6},{3,7},{4,0},{5,1},{6,2},{7,3},{8,12},{9,13},{10,... | collective-permute-start | bytes 1179656 | tf_op jit(solution)/shard_map/ppermute | solution.py:42
  20.4 18.8 %collective-permute-start.3 = (bf16[2048,192]{0,1:T(8,128)(2,1)S(1)}, bf16[2048,192]{0,1:T(8,128)(2,1)S(1)}, u32[]{:S(2)}, u32[]{:S(2)}) collective-permute-start(bf16[2048,192]{0,1:T(8,128)(2,1)S(1)} %maximum_select_fusion.2), channel_id=1, source_target_pairs={{0,8},{1,9},{2,10},{3,11},{4,12},{5,13},{6,14},{7,15},{8,0},{9,1},... | collective-permute-start | bytes 2359304 | tf_op jit(solution)/shard_map/ppermute | solution.py:42
  39.7 2.8 %copy-start = (bf16[4096,192]{0,1:T(8,128)(2,1)}, bf16[4096,192]{0,1:T(8,128)(2,1)S(1)}, u32[]{:S(2)}) copy-start(bf16[4096,192]{0,1:T(8,128)(2,1)S(1)} %maximum_select_fusion.1) | copy-start | bytes 4718596
  39.7 68.5 %collective-permute-start.4 = (bf16[4096,192]{0,1:T(8,128)(2,1)S(1)}, bf16[4096,192]{0,1:T(8,128)(2,1)}, u32[]{:S(2)}, u32[]{:S(2)}) collective-permute-start(bf16[4096,192]{0,1:T(8,128)(2,1)S(1)} %maximum_select_fusion.1), channel_id=1, source_target_pairs={{0,16},{1,17},{2,18},{3,19},{4,20},{5,21},{6,22},{7,23},{8,24},{9,... | collective-permute-start | bytes 4718600 | tf_op jit(solution)/shard_map/ppermute | solution.py:42
  115.8 21.1 %copy-start.1 = (f32[256,16]{0,1:T(8,128)S(1)}, f32[256,16]{0,1:T(8,128)}, u32[]{:S(2)}) copy-start(f32[256,16]{0,1:T(8,128)} %param.7) | copy-start | bytes 49156
